TPU v7x, 32 devices: a whole 2x2x4 slice. The times are simulated.
32 devices in a mesh: fsdp: 16 (over z, x, core), tp: 2 (over y).
Axes of the slice: x: 2, y: 2, z: 4, core: 2. Of those that a mesh axis runs over, the one named last changes fastest.
Arguments:
- grad_iterate: bfloat16 [3584, 18432], P('tp', 'fsdp'), may hold values from -0.036828478 to 0.036828478
Outputs:
- update: float32 [3584, 18432], P('tp', 'fsdp')
All inputs are finite; a program needn't handle non-finite values.
Results may differ from a plain program's by a relative error of at most 0.0031.
Values may be sent and summed in bfloat16 or wider, within the bound.
A program may use at most 128 MiB of HBM per device.

v0:
```python
import math

import jax
import jax.numpy as jnp
from jax import lax
from jax.sharding import PartitionSpec as P

C = 18432


quintic_one = 3.4445
quintic_three = -4.775
quintic_five = 2.0315


def local(grad_iterate):
    columns = lax.all_gather(grad_iterate, "tp", axis=0, tiled=True)
    shares = lax.psum_scatter(
        lax.dot_general(
            columns, grad_iterate, (((1,), (1,)), ((), ())), preferred_element_type=jnp.float32
        ),
        "fsdp",
        scatter_dimension=0,
        tiled=True,
    )
    gram_cols = lax.all_gather(shares.astype(jnp.bfloat16), "fsdp", axis=0, tiled=True)
    applied = lax.dot_general(
        gram_cols, columns, (((0,), (0,)), ((), ())), preferred_element_type=jnp.float32
    )
    applied_low = applied.astype(jnp.bfloat16)
    twice_applied = jnp.dot(
        gram_cols.T,
        lax.all_gather(applied_low, "tp", axis=0, tiled=True),
        preferred_element_type=jnp.float32,
    )
    mixed = (
        quintic_one * grad_iterate.astype(jnp.float32)
        + quintic_three * applied
        + quintic_five * twice_applied
    )
    return mixed * math.sqrt(C)


def solution(mesh):
    return jax.shard_map(
        local,
        mesh=mesh,
        in_specs=(P("tp", "fsdp"),),
        out_specs=P("tp", "fsdp"),
        check_vma=False,
    )
```

profile of v0, /device:TPU:0, one launch (start us, length us, event | category | flops | bytes accessed | tf_op | source)
XLA Modules:
  0.0 649.5 jit_solution(12908850568293151722)
XLA Ops:
  6.5 0.0 all-gather.4.cloned.1.call-start
  6.5 0.7 all-gather.4.cloned.1.call-update
  7.3 0.0 reduce-scatter.2.cloned.1.call-start
  7.3 106.8 %all-gather.4.cloned.1.call-done = bf16[3584,1152]{1,0:T(8,128)(2,1)} async-done(((bf16[1792,1152]{1,0:T(8,128)(2,1)}), bf16[3584,1152]{1,0:T(8,128)(2,1)}) %all-gather.4.cloned.1.call-update) | async-done | bytes 8257552 | tf_op jit(solution)/shard_map/all_gather | solution.py:17
  114.1 22.9 %fusion.3 = f32[3584,1792]{1,0:T(8,128)} fusion(bf16[3584,1152]{1,0:T(8,128)(2,1)} %all-gather.4.cloned.1.call-done, bf16[1792,1152]{1,0:T(8,128)(2,1)} %param.1), kind=kOutput, calls=%fused_computation.4 | convolution fusion | flops 14797504512 | bytes 38076416 | tf_op jit(solution)/shard_map/dot_general | solution.py:19
  137.0 0.0 reduce-scatter.2.cloned.1.call-update
  137.1 0.0 all-gather.6.cloned.1.call-start
  137.1 247.5 %reduce-scatter.2.cloned.1.call-done = f32[224,1792]{1,0:T(8,128)} async-done(((f32[3584,1792]{1,0:T(8,128)}), f32[224,1792]{1,0:T(8,128)}) %reduce-scatter.2.cloned.1.call-update) | async-done | bytes 1605648 | tf_op jit(solution)/shard_map/reduce_scatter | solution.py:18
  384.7 2.4 convert_element_type.10
  387.0 0.0 all-gather.6.cloned.1.call-update
  387.1 0.0 all-gather.8.cloned.1.call-start
  387.1 101.3 %all-gather.6.cloned.1.call-done = bf16[3584,1792]{1,0:T(8,128)(2,1)} async-done(((bf16[224,1792]{1,0:T(8,128)(2,1)}), bf16[3584,1792]{1,0:T(8,128)(2,1)}) %all-gather.6.cloned.1.call-update) | async-done | bytes 12845072 | tf_op jit(solution)/shard_map/all_gather | solution.py:26
  488.4 25.2 %fusion.2 = (bf16[1792,1152]{1,0:T(8,128)(2,1)}, f32[1792,1152]{1,0:T(8,128)}) fusion(bf16[3584,1792]{1,0:T(8,128)(2,1)} %all-gather.6.cloned.1.call-done, bf16[3584,1152]{1,0:T(8,128)(2,1)} %all-gather.4.cloned.1.call-done), kind=kOutput, calls=%fused_computation.3 | convolution fusion | flops 14799568896 | bytes 33488896 | tf_op jit(solution)/shard_map/dot_general | solution.py:27
  513.5 0.0 all-gather.8.cloned.1.call-update
  513.6 100.9 %all-gather.8.cloned.1.call-done = bf16[3584,1152]{1,0:T(8,128)(2,1)} async-done(((bf16[1792,1152]{1,0:T(8,128)(2,1)}), bf16[3584,1152]{1,0:T(8,128)(2,1)}) %all-gather.8.cloned.1.call-update) | async-done | bytes 8257552 | tf_op jit(solution)/shard_map/all_gather | solution.py:33
  614.5 28.5 %fusion.1 = f32[1792,1152]{1,0:T(8,128)} fusion(bf16[3584,1792]{1,0:T(8,128)(2,1)} %all-gather.6.cloned.1.call-done, bf16[3584,1152]{1,0:T(8,128)(2,1)} %all-gather.8.cloned.1.call-done, f32[1792,1152]{1,0:T(8,128)} %get-tuple-element.6, bf16[1792,1152]{1,0:T(8,128)(2,1)} %param.1), kind=kOutput, calls=%fused_computation.2 | convolution fusion | flops 14811955200 | bytes 41746432 | tf_op jit(solution)/shard_map/dot_general | solution.py:31
Async XLA Ops:
  6.5 107.6 %all-gather.4.cloned.1.call-start = ((), (), s32[]{:S(2)}) async-start(), calls=%async_computation.1 | async-start | bytes 12386304 | tf_op jit(solution)/shard_map/all_gather | solution.py:17
  7.3 377.4 %reduce-scatter.2.cloned.1.call-start = ((), (), s32[]{:S(2)}) async-start(), calls=%async_computation.2 | async-start | bytes 27295744 | tf_op jit(solution)/shard_map/reduce_scatter | solution.py:18
  137.1 351.3 %all-gather.6.cloned.1.call-start = ((), (), s32[]{:S(2)}) async-start(), calls=%async_computation.3 | async-start | bytes 13647872 | tf_op jit(solution)/shard_map/all_gather | solution.py:26
  387.1 227.4 %all-gather.8.cloned.1.call-start = ((), (), s32[]{:S(2)}) async-start(), calls=%async_computation.4 | async-start | bytes 12386304 | tf_op jit(solution)/shard_map/all_gather | solution.py:33
Sparse Core Ops, SparseCore 0:
  8.9 105.2 all-gather.3
  137.2 247.4 reduce-scatter.1
  387.2 101.1 all-gather.5
  513.7 100.7 all-gather.7
where the time goes:
time: 650 us; the launch traced here: 649 us
  waiting for transfers between devices  557 us (86%)
  matrix products  76.5 us (12%)
  between operations  13.1 us (2%)
    reduce_scatter x1, waiting for transfers between devices, local(): lax.psum_scatter(lax.dot_general(columns, grad_iterate, (((1,), (1,)), ((...  248 us
    all_gather x1, waiting for transfers between devices, local(): columns = lax.all_gather(grad_iterate, 'tp', axis=0, tiled=True)  107 us
    all_gather x1, waiting for transfers between devices, local(): lax.all_gather(shares.astype(jnp.bfloat16), 'fsdp', axis=0, tiled=True)  101 us
    all_gather x1, waiting for transfers between devices, local(): lax.all_gather(applied_low, 'tp', axis=0, tiled=True)  101 us
    dot_general x1, matrix products, local(): jnp.dot(gram_cols.T, lax.all_gather(applied_low, 'tp', axis=0, tiled=True...  28.5 us
    dot_general x1, matrix products, local(): lax.dot_general(gram_cols, columns, (((0,), (0,)), ((), ())), preferred_e...  25.2 us
    dot_general x1, matrix products, local(): lax.dot_general(columns, grad_iterate, (((1,), (1,)), ((), ())), preferre...  22.9 us
  transfers between devices with their start and end apart: 4, of which 4 were waited for; matrix products, arithmetic and copies ran while one was open for 0% of the time, Pallas kernels for 0%

commit v1 on v0

v1 whole, which is shorter than its diff:
```python
import functools
import math

import jax
import jax.numpy as jnp
from jax import lax
from jax.sharding import PartitionSpec as P

C = 18432


quintic_one = 3.4445
quintic_three = -4.775
quintic_five = 2.0315


def rows_by_rows(a, b):
    return lax.dot_general(a, b, (((1,), (1,)), ((), ())), preferred_element_type=jnp.float32)


def matmul(a, b):
    return jnp.dot(a, b, preferred_element_type=jnp.float32)


def general(grad_iterate):
    columns = lax.all_gather(grad_iterate, "tp", axis=0, tiled=True)
    shares = lax.psum_scatter(
        rows_by_rows(columns, grad_iterate), "fsdp", scatter_dimension=0, tiled=True
    )
    gram_cols = lax.all_gather(shares.astype(jnp.bfloat16), "fsdp", axis=0, tiled=True)
    applied = lax.dot_general(
        gram_cols, columns, (((0,), (0,)), ((), ())), preferred_element_type=jnp.float32
    )
    twice_applied = matmul(
        gram_cols.T, lax.all_gather(applied.astype(jnp.bfloat16), "tp", axis=0, tiled=True)
    )
    mixed = (
        quintic_one * grad_iterate.astype(jnp.float32)
        + quintic_three * applied
        + quintic_five * twice_applied
    )
    return mixed * math.sqrt(C)


def chunks_of(width):
    for count in (3, 2):
        if width % (count * 128) == 0:
            return count
    return 1


def paired(devices, own):
    rows, width = own.shape
    half = rows // 2
    piece = rows // (2 * devices)
    swap = [(0, 1), (1, 0)]
    first = lax.axis_index("tp") == 0

    def reduced(partial):
        share = lax.psum_scatter(partial, "fsdp", scatter_dimension=0, tiled=True)
        return share.astype(jnp.bfloat16)

    other = lax.ppermute(own, "tp", swap)

    left_share = reduced(rows_by_rows(own, own[:half]))
    corner_share = reduced(rows_by_rows(own[half:], own[half:]))

    picked = jnp.where(
        first,
        other.reshape(devices, 2, piece, width)[:, 0],
        own.reshape(devices, 2, piece, width)[:, 1],
    ).reshape(half, width)
    cross_share = reduced(rows_by_rows(picked, jnp.where(first, own, other)))
    cross_share = lax.all_gather(cross_share, "tp", axis=0, tiled=True)

    left = lax.all_gather(left_share, "fsdp", axis=0, tiled=True)
    corner = lax.all_gather(corner_share, "fsdp", axis=0, tiled=True)
    diagonal = jnp.concatenate(
        [left, jnp.concatenate([left[half:].T, corner], axis=0)], axis=1
    )
    cross = lax.all_gather(cross_share, "fsdp", axis=0, tiled=True)
    cross = jnp.where(first, cross.T, cross)

    count = chunks_of(width)
    step = width // count
    spans = [slice(i * step, (i + 1) * step) for i in range(count)]
    applied = [matmul(diagonal, own[:, s]) + matmul(cross, other[:, s]) for s in spans]
    low = [a.astype(jnp.bfloat16) for a in applied]
    far = [lax.ppermute(a, "tp", swap) for a in low]
    near = [matmul(diagonal, a) for a in low]
    out = []
    for i, s in enumerate(spans):
        twice = near[i] + matmul(cross, far[i])
        mixed = (
            quintic_one * own[:, s].astype(jnp.float32)
            + quintic_three * applied[i]
            + quintic_five * twice
        )
        out.append(mixed * math.sqrt(C))
    return jnp.concatenate(out, axis=1)


def solution(mesh):
    devices = mesh.shape["fsdp"]
    pair = mesh.shape["tp"] == 2

    def local(grad_iterate):
        if pair and grad_iterate.shape[0] % (2 * devices) == 0:
            return paired(devices, grad_iterate)
        return general(grad_iterate)

    return jax.shard_map(
        local,
        mesh=mesh,
        in_specs=(P("tp", "fsdp"),),
        out_specs=P("tp", "fsdp"),
        check_vma=False,
    )
```

time: 650 us -> 563 us (0.87); the launches traced: 649 us -> 556 us
  waiting for transfers between devices: 557 us -> 359 us
  matrix products: 76.5 us -> 118 us
  local copies, waits for them, and re-layouts: 0 us -> 33.1 us
  other arithmetic: 2.38 us -> 16.6 us
  starting transfers between devices: 0.12 us -> 8.54 us
  blocking collectives: 0 us -> 6.95 us
    all_gather x3, waiting for transfers between devices: 309 us -> 112 us  [the longest x1 46.5 us: paired(): cross = lax.all_gather(cross_share, 'fsdp', axis=0, tiled=True)]
    reduce_scatter x1 -> x2, waiting for transfers between devices: 248 us -> 87.4 us  [reduced(): share = lax.psum_scatter(partial, 'fsdp', scatter_dimension=0, tiled=True)]
    ppermute x0 -> x4, waiting for transfers between devices: none -> 104 us  [the longest x1 83.1 us: paired(): other = lax.ppermute(own, 'tp', swap)]
    unnamed x4 -> x7, waiting for transfers between devices: 0.76 us -> 55.6 us
    dot_general x3 -> x15, matrix products: 76.5 us -> 118 us  [the longest x12 94.5 us: matmul(): return jnp.dot(a, b, preferred_element_type=jnp.float32)]
    unnamed x0 -> x35, local copies, waits for them, and re-layouts: none -> 12.8 us
    all_gather x0 -> x1, local copies, waits for them, and re-layouts: none -> 9.98 us  [paired(): cross = lax.all_gather(cross_share, 'fsdp', axis=0, tiled=True)]
    concatenate x0 -> x1, local copies, waits for them, and re-layouts: none -> 8.85 us  [paired(): return jnp.concatenate(out, axis=1)]
  transfers between devices with their start and end apart: 4 -> 10, of which waited for: 4 -> 7; matrix products, arithmetic and copies ran while one was open for 0% -> 21% of each run, Pallas kernels for 0% -> 0%
where the time goes in v1:
time: 563 us; the launch traced here: 556 us
  waiting for transfers between devices  359 us (64%)
  matrix products  118 us (21%)
  local copies, waits for them, and re-layouts  33.1 us (6%)
  other arithmetic  16.6 us (3%)
  between operations  13.9 us (2%)
  starting transfers between devices  8.54 us (2%)
  blocking collectives  6.95 us (1%)
    dot_general x12, matrix products, matmul(): return jnp.dot(a, b, preferred_element_type=jnp.float32)  94.5 us
    reduce_scatter x2, waiting for transfers between devices, reduced(): share = lax.psum_scatter(partial, 'fsdp', scatter_dimension=0, tiled=True)  87.4 us
    ppermute x1, waiting for transfers between devices, paired(): other = lax.ppermute(own, 'tp', swap)  83.1 us
    unnamed x7, waiting for transfers between devices  55.6 us
    all_gather x1, waiting for transfers between devices, paired(): cross = lax.all_gather(cross_share, 'fsdp', axis=0, tiled=True)  46.5 us
    all_gather x1, waiting for transfers between devices, paired(): corner = lax.all_gather(corner_share, 'fsdp', axis=0, tiled=True)  36.3 us
    all_gather x1, waiting for transfers between devices, paired(): left = lax.all_gather(left_share, 'fsdp', axis=0, tiled=True)  29.3 us
    dot_general x3, matrix products, rows_by_rows(): lax.dot_general(a, b, (((1,), (1,)), ((), ())), preferred_element_type=jn...  23.3 us
  transfers between devices with their start and end apart: 10, of which 7 were waited for; matrix products, arithmetic and copies ran while one was open for 21% of the time, Pallas kernels for 0%

profile of v1, /device:TPU:0, one launch (start us, length us, event | category | flops | bytes accessed | tf_op | source)
XLA Modules:
  0.0 555.7 jit_solution(13139247162025827451)
XLA Ops:
  6.5 10.4 %fusion.14 = f32[1792,896]{1,0:T(8,128)} fusion(bf16[1792,1152]{1,0:T(8,128)(2,1)} %param.1), kind=kOutput, calls=%fused_computation.24 | convolution fusion | flops 3699376128 | bytes 12615680 | tf_op jit(solution)/shard_map/dot_general | solution.py:18
  17.0 0.0 reduce-scatter.10.cloned.1.call-start
  17.0 3.1 collective-permute-start
  20.1 6.3 %fusion.12 = f32[896,896]{1,0:T(8,128)} fusion(bf16[1792,1152]{1,0:T(8,128)(2,1)} %param.1), kind=kOutput, calls=%fused_computation.22 | convolution fusion | flops 1849688064 | bytes 5275648 | tf_op jit(solution)/shard_map/dot_general | solution.py:18
  26.4 0.0 reduce-scatter.8.cloned.1.call-start
  26.5 83.1 %collective-permute-done = bf16[1792,1152]{1,0:T(8,128)(2,1)} collective-permute-done((bf16[1792,1152]{1,0:T(8,128)(2,1)}, bf16[1792,1152]{1,0:T(8,128)(2,1)}, u32[]{:S(2)}, u32[]{:S(2)}) %collective-permute-start) | collective-permute-done | bytes 4128800 | tf_op jit(solution)/shard_map/ppermute | solution.py:63
  109.6 2.6 slice_select_fusion
  112.2 0.8 copy-done
  113.0 6.5 %fusion = f32[896,1792]{1,0:T(8,128)} fusion(bf16[896,1152]{1,0:T(8,128)(2,1)S(1)} %bitcast.22, bf16[1792,1152]{1,0:T(8,128)(2,1)S(1)} %copy-done, bf16[1792,1152]{1,0:T(8,128)(2,1)} %collective-permute-done, pred[]{:T(512)S(6)} %eq.3), kind=kOutput, calls=%fused_computation.3 | convolution fusion | flops 3701440512 | bytes 16744449 | tf_op jit(solution)/shard_map/dot_general | solution.py:18
  119.5 0.0 all-gather.4.cloned.1.call-start
  119.6 0.0 reduce-scatter.6.cloned.1.call-done
  119.6 1.7 convert_element_type.28
  121.3 0.0 all-gather.6.cloned.1.call-start
  121.4 55.5 %reduce-scatter.10.cloned.1.call-done = f32[56,896]{1,0:T(8,128)} async-done(((f32[896,896]{1,0:T(8,128)}), f32[56,896]{1,0:T(8,128)}) %reduce-scatter.10.cloned.1.call-update) | async-done | bytes 200720
  176.8 1.6 convert_element_type.29
  178.4 0.0 all-gather.8.cloned.1.call-start
  178.5 87.4 %reduce-scatter.8.cloned.1.call-done = f32[56,1792]{1,0:T(8,128)} async-done(((f32[896,1792]{1,0:T(8,128)}), f32[56,1792]{1,0:T(8,128)}) %reduce-scatter.8.cloned.1.call-update) | async-done | bytes 401424 | tf_op jit(solution)/shard_map/reduce_scatter | solution.py:60
  265.9 1.0 convert_element_type.30
  266.9 7.0 %all_gather.14 = bf16[112,1792]{1,0:T(8,128)(2,1)} all-gather(bf16[56,1792]{1,0:T(8,128)(2,1)S(1)} %convert_element_type.30), channel_id=1, replica_groups=mesh['fsdp'=16,'tp'=2] {'tp'}, dimensions={0}, use_global_device_ids=true | all-gather | bytes 602112 | tf_op jit(solution)/shard_map/all_gather | solution.py:74
  273.9 0.0 all-gather.8.cloned.1.call-update
  273.9 3.8 fusion.28
  277.7 2.5 copy.14
  280.3 1.6 copy.16
  281.9 1.6 copy.17
  283.5 29.3 %all-gather.4.cloned.1.call-done = bf16[1792,896]{1,0:T(8,128)(2,1)} async-done(((bf16[112,896]{1,0:T(8,128)(2,1)}), bf16[1792,896]{1,0:T(8,128)(2,1)}) %all-gather.4.cloned.1.call-update) | async-done | bytes 3211280 | tf_op jit(solution)/shard_map/all_gather | solution.py:76
  312.7 1.4 slice-done
  314.2 2.3 copy.15
  316.5 36.3 %all-gather.6.cloned.1.call-done = bf16[896,896]{1,0:T(8,128)(2,1)} async-done(((bf16[56,896]{1,0:T(8,128)(2,1)}), bf16[896,896]{1,0:T(8,128)(2,1)}) %all-gather.6.cloned.1.call-update) | async-done | bytes 1605648 | tf_op jit(solution)/shard_map/all_gather | solution.py:77
  352.8 7.6 %fusion.21 = f32[1792,384]{0,1:T(8,128)} fusion(bf16[1792,1152]{1,0:T(8,128)(2,1)} %param.1, bf16[896,896]{1,0:T(8,128)(2,1)} %all-gather.6.cloned.1.call-done, bf16[896,896]{1,0:T(8,128)(2,1)} %bitcast.23, bf16[1792,896]{1,0:T(8,128)(2,1)} %all-gather.4.cloned.1.call-done), kind=kOutput, calls=%fused_computation.31 | convolution fusion | flops 2485518336 | bytes 10551296 | tf_op jit(solution)/shard_map/dot_general | solution.py:22
  360.5 4.3 fusion.19
  364.8 4.5 fusion.23
  369.2 46.5 %all-gather.8.cloned.1.call-done = bf16[1792,1792]{1,0:T(8,128)(2,1)} async-done(((bf16[112,1792]{1,0:T(8,128)(2,1)}), bf16[1792,1792]{1,0:T(8,128)(2,1)}) %all-gather.8.cloned.1.call-update) | async-done | bytes 6422544 | tf_op jit(solution)/shard_map/all_gather | solution.py:81
  415.8 10.0 %copy.10 = bf16[1792,1792]{0,1:T(8,128)(2,1)} copy(bf16[1792,1792]{1,0:T(8,128)(2,1)} %all-gather.8.cloned.1.call-done) | data formatting | bytes 12845056 | tf_op jit(solution)/shard_map/all_gather | solution.py:81
  425.7 6.2 %bitcast_select_fusion = bf16[1792,1792]{1,0:T(8,128)(2,1)} fusion(bf16[1792,1792]{1,0:T(8,128)(2,1)} %all-gather.8.cloned.1.call-done, bf16[1792,1792]{0,1:T(8,128)(2,1)} %copy.10, pred[]{:T(512)S(6)} %eq.3), kind=kLoop, calls=%fused_computation.2 | loop fusion | flops 3211264 | bytes 19267584 | tf_op jit(solution)/shard_map/jit(_where)/select_n | solution.py:82
  432.0 8.4 %fusion.30 = (bf16[1792,384]{0,1:T(8,128)(2,1)S(1)}, f32[1792,384]{0,1:T(8,128)}) fusion(f32[1792,384]{0,1:T(8,128)} %fusion.21, bf16[1792,1792]{1,0:T(8,128)(2,1)} %bitcast_select_fusion, bf16[1792,1152]{1,0:T(8,128)(2,1)} %collective-permute-done), kind=kOutput, calls=%fused_computation.40 | convolution fusion | flops 2467627008 | bytes 14680064 | tf_op jit(solution)/shard_map/dot_general | solution.py:22
  440.4 3.3 collective-permute-start.2
  443.8 5.6 %fusion.29 = (bf16[1792,384]{0,1:T(8,128)(2,1)S(1)}, f32[1792,384]{0,1:T(8,128)}) fusion(f32[1792,384]{0,1:T(8,128)S(1)} %copy-done.14, bf16[1792,1792]{1,0:T(8,128)(2,1)S(1)} %copy-done.2, bf16[1792,1152]{1,0:T(8,128)(2,1)} %collective-permute-done), kind=kOutput, calls=%fused_computation.39 | convolution fusion | flops 2467627008 | bytes 14680064 | tf_op jit(solution)/shard_map/dot_general | solution.py:22
  449.4 5.1 fusion.31
  454.5 1.9 collective-permute-start.1
  456.4 15.4 %fusion.26 = f32[1792,384]{0,1:T(8,128)} fusion(bf16[1792,384]{0,1:T(8,128)(2,1)S(1)} %get-tuple-element.10, bf16[896,896]{1,0:T(8,128)(2,1)S(1)} %copy-done.10, bf16[896,896]{1,0:T(8,128)(2,1)S(1)} %bitcast.26, bf16[1792,896]{1,0:T(8,128)(2,1)S(1)} %copy-done.3), kind=kOutput, calls=%fused_computation.36 | convolution fusion | flops 2485518336 | bytes 10551296 | tf_op jit(solution)/shard_map/dot_general | solution.py:22
  471.8 15.6 %fusion.25 = f32[1792,384]{0,1:T(8,128)} fusion(bf16[1792,384]{0,1:T(8,128)(2,1)S(1)} %get-tuple-element.8, bf16[896,896]{1,0:T(8,128)(2,1)S(1)} %copy-done.10, bf16[896,896]{1,0:T(8,128)(2,1)S(1)} %bitcast.27, bf16[1792,896]{1,0:T(8,128)(2,1)S(1)} %copy-done.3), kind=kOutput, calls=%fused_computation.35 | convolution fusion | flops 2485518336 | bytes 10551296 | tf_op jit(solution)/shard_map/dot_general | solution.py:22
  487.4 15.3 %fusion.27 = f32[1792,384]{0,1:T(8,128)} fusion(bf16[1792,384]{0,1:T(8,128)(2,1)S(1)} %get-tuple-element.12, bf16[896,896]{1,0:T(8,128)(2,1)S(1)} %copy-done.10, bf16[896,896]{1,0:T(8,128)(2,1)S(1)} %bitcast.28, bf16[1792,896]{1,0:T(8,128)(2,1)S(1)} %copy-done.3), kind=kOutput, calls=%fused_computation.37 | convolution fusion | flops 2485518336 | bytes 10551296 | tf_op jit(solution)/shard_map/dot_general | solution.py:22
  502.8 6.7 %fusion.8 = f32[1792,384]{0,1:T(8,128)S(1)} fusion(f32[1792,384]{0,1:T(8,128)} %fusion.26, bf16[1792,1792]{1,0:T(8,128)(2,1)S(1)} %copy-done.2, bf16[1792,384]{0,1:T(8,128)(2,1)S(1)} %collective-permute-done.2, f32[1792,384]{0,1:T(8,128)} %get-tuple-element.11, bf16[1792,384]{0,1:T(8,128)(2,1)S(1)} %copy-done.8), kind=kOutput, calls=%fused_computation.14 | convolution fusion | flops 2471755776 | bytes 17432576 | tf_op jit(solution)/shard_map/dot_general | solution.py:22
  509.6 3.0 fusion.5
  512.5 20.8 %collective-permute-done.1 = bf16[1792,384]{0,1:T(8,128)(2,1)S(1)} collective-permute-done((bf16[1792,384]{0,1:T(8,128)(2,1)S(1)}, bf16[1792,384]{0,1:T(8,128)(2,1)S(1)}, u32[]{:S(2)}, u32[]{:S(2)}) %collective-permute-start.1) | collective-permute-done | bytes 1376288 | tf_op jit(solution)/shard_map/ppermute | solution.py:89
  533.4 2.9 fusion.11
  536.3 3.5 pad_maximum_fusion
  539.8 8.8 %copy.13 = f32[1792,1152]{1,0:T(8,128)} copy(f32[1792,1152]{0,1:T(8,128)} %pad_maximum_fusion) | data formatting | bytes 16515072 | tf_op jit(solution)/shard_map/concatenate | solution.py:100
  (39 shorter events, 0.2 us)
Async XLA Ops:
  6.5 113.1 %reduce-scatter.6.cloned.1.call-start = ((), (), s32[]{:S(2)}) async-start(), calls=%async_computation.3 | async-start | bytes 6823936 | tf_op jit(solution)/shard_map/reduce_scatter | solution.py:60
  17.0 159.9 %reduce-scatter.10.cloned.1.call-start = ((), (), s32[]{:S(2)}) async-start(), calls=%async_computation.8 | async-start | bytes 3411968
  17.0 92.5 %collective-permute-start = (bf16[1792,1152]{1,0:T(8,128)(2,1)}, bf16[1792,1152]{1,0:T(8,128)(2,1)}, u32[]{:S(2)}, u32[]{:S(2)}) collective-permute-start(bf16[1792,1152]{1,0:T(8,128)(2,1)} %param.1), channel_id=1, source_target_pairs={{0,1},{1,0},{2,3},{3,2},{4,5},{5,4},{6,7},{7,6},{8,9},{9,8},{10,11... | collective-permute-start | bytes 12386312 | tf_op jit(solution)/shard_map/ppermute | solution.py:63
  26.4 239.4 %reduce-scatter.8.cloned.1.call-start = ((), (), s32[]{:S(2)}) async-start(), calls=%async_computation.6 | async-start | bytes 6823936 | tf_op jit(solution)/shard_map/reduce_scatter | solution.py:60
  109.6 3.4 copy-start
  119.5 193.2 %all-gather.4.cloned.1.call-start = ((), (), s32[]{:S(2)}) async-start(), calls=%async_computation.4 | async-start | bytes 3411968 | tf_op jit(solution)/shard_map/all_gather | solution.py:76
  121.3 231.5 %all-gather.6.cloned.1.call-start = ((), (), s32[]{:S(2)}) async-start(), calls=%async_computation.5 | async-start | bytes 1705984 | tf_op jit(solution)/shard_map/all_gather | solution.py:77
  178.4 237.3 %all-gather.8.cloned.1.call-start = ((), (), s32[]{:S(2)}) async-start(), calls=%async_computation.7 | async-start | bytes 6823936 | tf_op jit(solution)/shard_map/all_gather | solution.py:81
  312.7 1.4 slice-start
  352.8 7.6 %copy-start.1 = (bf16[1792,1152]{1,0:T(8,128)(2,1)S(1)}, bf16[1792,1152]{1,0:T(8,128)(2,1)}, u32[]{:S(2)}) copy-start(bf16[1792,1152]{1,0:T(8,128)(2,1)} %param.1) | copy-start | bytes 12386308
  352.8 7.6 %copy-start.3 = (bf16[1792,896]{1,0:T(8,128)(2,1)S(1)}, bf16[1792,896]{1,0:T(8,128)(2,1)}, u32[]{:S(2)}) copy-start(bf16[1792,896]{1,0:T(8,128)(2,1)} %all-gather.4.cloned.1.call-done) | copy-start | bytes 9633796
  352.8 7.6 %copy-start.4 = (bf16[896,896]{0,1:T(8,128)(2,1)S(1)}, bf16[896,896]{0,1:T(8,128)(2,1)}, u32[]{:S(2)}) copy-start(bf16[896,896]{0,1:T(8,128)(2,1)} %copy.15) | copy-start | bytes 4816900
  352.8 7.6 %copy-start.9 = (bf16[896,896]{1,0:T(8,128)(2,1)S(1)}, bf16[896,896]{1,0:T(8,128)(2,1)}, u32[]{:S(2)}) copy-start(bf16[896,896]{1,0:T(8,128)(2,1)} %all-gather.6.cloned.1.call-done) | copy-start | bytes 4816900
  432.0 11.8 %copy-start.2 = (bf16[1792,1792]{1,0:T(8,128)(2,1)S(1)}, bf16[1792,1792]{1,0:T(8,128)(2,1)}, u32[]{:S(2)}) copy-start(bf16[1792,1792]{1,0:T(8,128)(2,1)} %bitcast_select_fusion) | copy-start | bytes 19267588
  432.0 11.8 %copy-start.14 = (f32[1792,384]{0,1:T(8,128)S(1)}, f32[1792,384]{0,1:T(8,128)}, u32[]{:S(2)}) copy-start(f32[1792,384]{0,1:T(8,128)} %fusion.19) | copy-start | bytes 8257540
  440.4 62.3 %collective-permute-start.2 = (bf16[1792,384]{0,1:T(8,128)(2,1)S(1)}, bf16[1792,384]{0,1:T(8,128)(2,1)S(1)}, u32[]{:S(2)}, u32[]{:S(2)}) collective-permute-start(bf16[1792,384]{0,1:T(8,128)(2,1)S(1)} %get-tuple-element.10), channel_id=1, source_target_pairs={{0,1},{1,0},{2,3},{3,2},{4,5},{5,4},{6,7},{7,6},{8,9},{9,8},{10,11... | collective-permute-start | bytes 4128776 | tf_op jit(solution)/shard_map/ppermute | solution.py:89
  449.4 7.0 %copy-start.5 = (bf16[896,896]{0,1:T(8,128)(2,1)S(1)}, bf16[896,896]{0,1:T(8,128)(2,1)}, u32[]{:S(2)}) copy-start(bf16[896,896]{0,1:T(8,128)(2,1)} %copy.15) | copy-start | bytes 4816900
  449.4 7.0 %copy-start.10 = (bf16[896,896]{1,0:T(8,128)(2,1)S(1)}, bf16[896,896]{1,0:T(8,128)(2,1)}, u32[]{:S(2)}) copy-start(bf16[896,896]{1,0:T(8,128)(2,1)} %all-gather.6.cloned.1.call-done) | copy-start | bytes 4816900
  449.4 60.1 %collective-permute-start.3 = (bf16[1792,384]{0,1:T(8,128)(2,1)S(1)}, bf16[1792,384]{0,1:T(8,128)(2,1)S(1)}, u32[]{:S(2)}, u32[]{:S(2)}) collective-permute-start(bf16[1792,384]{0,1:T(8,128)(2,1)S(1)} %get-tuple-element.8), channel_id=1, source_target_pairs={{0,1},{1,0},{2,3},{3,2},{4,5},{5,4},{6,7},{7,6},{8,9},{9,8},{10,11... | collective-permute-start | bytes 4128776 | tf_op jit(solution)/shard_map/ppermute | solution.py:89
  454.5 78.9 %collective-permute-start.1 = (bf16[1792,384]{0,1:T(8,128)(2,1)S(1)}, bf16[1792,384]{0,1:T(8,128)(2,1)S(1)}, u32[]{:S(2)}, u32[]{:S(2)}) collective-permute-start(bf16[1792,384]{0,1:T(8,128)(2,1)S(1)} %get-tuple-element.12), channel_id=1, source_target_pairs={{0,1},{1,0},{2,3},{3,2},{4,5},{5,4},{6,7},{7,6},{8,9},{9,8},{10,11... | collective-permute-start | bytes 4128776 | tf_op jit(solution)/shard_map/ppermute | solution.py:89
  487.4 15.3 %copy-start.8 = (bf16[1792,384]{0,1:T(8,128)(2,1)S(1)}, bf16[1792,384]{0,1:T(8,128)(2,1)}, u32[]{:S(2)}) copy-start(bf16[1792,384]{0,1:T(8,128)(2,1)} %copy.16) | copy-start | bytes 4128772
  502.7 6.8 %copy-start.7 = (bf16[1792,384]{0,1:T(8,128)(2,1)S(1)}, bf16[1792,384]{0,1:T(8,128)(2,1)}, u32[]{:S(2)}) copy-start(bf16[1792,384]{0,1:T(8,128)(2,1)} %copy.17) | copy-start | bytes 4128772
  502.7 6.8 %copy-start.11 = (f32[1792,384]{0,1:T(8,128)S(1)}, f32[1792,384]{0,1:T(8,128)}, u32[]{:S(2)}) copy-start(f32[1792,384]{0,1:T(8,128)} %get-tuple-element.9) | copy-start | bytes 8257540
  502.8 6.8 %copy-start.13 = (f32[1792,384]{0,1:T(8,128)S(1)}, f32[1792,384]{0,1:T(8,128)}, u32[]{:S(2)}) copy-start(f32[1792,384]{0,1:T(8,128)} %fusion.25) | copy-start | bytes 8257540
  509.5 23.8 %copy-start.6 = (bf16[1792,384]{0,1:T(8,128)(2,1)S(1)}, bf16[1792,384]{0,1:T(8,128)(2,1)}, u32[]{:S(2)}) copy-start(bf16[1792,384]{0,1:T(8,128)(2,1)} %copy.14) | copy-start | bytes 4128772
  509.5 23.8 %copy-start.12 = (f32[1792,384]{0,1:T(8,128)S(1)}, f32[1792,384]{0,1:T(8,128)}, u32[]{:S(2)}) copy-start(f32[1792,384]{0,1:T(8,128)} %fusion.27) | copy-start | bytes 8257540
Sparse Core Ops, SparseCore 0:
  17.1 88.8 reduce-scatter.5
  109.8 66.9 reduce-scatter.9
  180.8 85.0 reduce-scatter.7
  267.9 44.7 all-gather.3
  314.7 38.0 all-gather.5
  355.0 60.7 all-gather.7
